TPU v7x, 32 devices: a whole 2x2x4 slice. The times are simulated.
32 devices in a mesh: row: 8 (over y, x, core), col: 4 (over z).
Axes of the slice: x: 2, y: 2, z: 4, core: 2. Of those that a mesh axis runs over, the one named last changes fastest.
Arguments:
- schur_tail: float32 [1024, 1024], P(('row', 'col')), as said below
- coupling: float32 [1024, 16384], P(None, 'row'), may hold values from -4 to 4
- ks_lead: float32 [16384, 4096], P('row', 'col'), may hold values from -0.046875 to 0.046875
- ks_tail: float32 [1024, 4096], P('row', 'col'), may hold values from -0.046875 to 0.046875
- inv_mask: int32 [8, 136], replicated, may hold values 0 or 1
- ks_mask: int32 [136, 32], replicated, may hold values 0 or 1
Outputs:
- projected: float32 [1024, 4096], P('row', 'col')
Inputs may be any that keep to these rules, and one draw needn't show every extreme that they name: `schur_tail`: symmetric and positive definite, with diagonal entries between about 1 and 32.
All inputs are finite; a program needn't handle non-finite values.
Results may differ from a plain program's by a relative error of at most 0.00009.
Values sent between devices are 32-bit elements; how exact they have to be, the bound alone decides.
A program may use at most 128 MiB of HBM per device.

v0:
```python
import jax
import jax.numpy as jnp
from jax import lax
from jax.sharding import PartitionSpec as P

BLK = 128


def expand(block_mask):
    widened = jnp.repeat(block_mask.astype(jnp.float32), BLK, axis=0)
    return jnp.repeat(widened, BLK, axis=1)


def product(left_rows, right_rows):
    return jnp.dot(
        left_rows, right_rows, precision=lax.Precision.HIGHEST, preferred_element_type=jnp.float32
    )


def per_device(schur_tail, coupling, ks_lead, ks_tail, inv_mask, ks_mask):
    row_index = lax.axis_index("row")
    col_index = lax.axis_index("col")
    gathered = lax.all_gather(schur_tail, ("row", "col"), axis=0, tiled=True)
    tail_size = gathered.shape[0]
    factor = jnp.linalg.cholesky(gathered)
    identity = jnp.eye(tail_size, dtype=jnp.float32)
    tail_inv = jax.scipy.linalg.solve_triangular(factor, identity, lower=True)
    lead_width = coupling.shape[1]
    lead_blocks = lead_width // BLK
    col_width = ks_lead.shape[1]
    col_blocks = col_width // BLK
    tail_rows = ks_tail.shape[0]
    lead_total_blocks = inv_mask.shape[1] - tail_size // BLK
    lead_mask = expand(lax.dynamic_slice_in_dim(inv_mask, row_index * lead_blocks, lead_blocks, 1))
    lead_part = -product(tail_inv, coupling) * lead_mask
    lead_ks_mask = expand(
        lax.dynamic_slice(
            ks_mask, (row_index * lead_blocks, col_index * col_blocks), (lead_blocks, col_blocks)
        )
    )
    ks_block = ks_lead * lead_ks_mask
    tail_ks_mask = expand(
        lax.dynamic_slice(
            ks_mask, (lead_total_blocks, col_index * col_blocks), (tail_size // BLK, col_blocks)
        )
    )
    masked_inv = tail_inv * expand(inv_mask[:, lead_total_blocks:])
    own_tail_mask = lax.dynamic_slice_in_dim(tail_ks_mask, row_index * tail_rows, tail_rows, 0)
    tail_block = ks_tail * own_tail_mask
    diag_cols = lax.dynamic_slice_in_dim(masked_inv, row_index * tail_rows, tail_rows, 1)
    return lax.psum_scatter(
        product(lead_part, ks_block) + product(diag_cols, tail_block),
        "row",
        scatter_dimension=0,
        tiled=True,
    )


def solution(mesh):
    in_specs = (P(("row", "col"), None), P(None, "row"), P("row", "col"), P("row", "col"), P(), P())
    out_specs = P("row", "col")
    return jax.shard_map(
        per_device, mesh=mesh, in_specs=in_specs, out_specs=out_specs, check_vma=False
    )
```

profile of v0, /device:TPU:0, one launch (start us, length us, event | category | flops | bytes accessed | tf_op | source)
XLA Modules:
  0.0 552.4 jit_solution(15435721150416295025)
XLA Ops:
  10.0 2.4 fusion.25
  14.8 5.3 copy_bitcast_fusion
  20.1 54.6 %all-gather.2.cloned.1.call-done = f32[1024,1024]{1,0:T(8,128)} async-done(((f32[32,1024]{1,0:T(8,128)}), f32[1024,1024]{1,0:T(8,128)}) %all-gather.2.cloned.1.call-update) | async-done | bytes 4194320 | tf_op jit(solution)/shard_map/all_gather | solution.py:23
  74.7 5.9 %copy.11 = f32[1024,1024]{0,1:T(8,128)} copy(f32[1024,1024]{1,0:T(8,128)} %all-gather.2.cloned.1.call-done) | data formatting | bytes 8388608 | tf_op jit(solution)/shard_map/all_gather | solution.py:23
  80.6 4.4 fusion.4
  87.0 11.7 %cholesky.223 = f32[128,128]{1,0:T(8,128)S(1)} custom-call(f32[128,128]{1,0:T(8,128)S(1)} %cholesky.580), custom_call_target="Cholesky" | custom-call | tf_op jit(solution)/shard_map/jit(cholesky)/cholesky | solution.py:25
  98.7 9.8 %custom-call.63 = f32[1,128,128]{1,2,0:T(8,128)S(1)} custom-call(f32[1,128,128]{2,1,0:T(8,128)S(1)} %get-tuple-element.69), custom_call_target="InvertDiagBlocksLowerTriangular" | custom-call | tf_op jit(solution)/shard_map/jit(cholesky)/cholesky | solution.py:25
  108.6 2.5 cholesky.255
  111.0 2.3 constant_dynamic-update-slice_fusion.25
  114.9 11.9 %cholesky.244 = f32[128,128]{1,0:T(8,128)S(1)} custom-call(f32[128,128]{1,0:T(8,128)S(1)} %cholesky.584), custom_call_target="Cholesky" | custom-call | tf_op jit(solution)/shard_map/jit(cholesky)/cholesky | solution.py:25
  127.4 9.8 %custom-call.64 = f32[1,128,128]{1,2,0:T(8,128)S(1)} custom-call(f32[1,128,128]{2,1,0:T(8,128)S(1)} %get-tuple-element.66), custom_call_target="InvertDiagBlocksLowerTriangular" | custom-call | tf_op jit(solution)/shard_map/jit(cholesky)/cholesky | solution.py:25
  140.6 11.7 %cholesky.468 = f32[128,128]{1,0:T(8,128)S(1)} custom-call(f32[128,128]{1,0:T(8,128)S(1)} %cholesky.589), custom_call_target="Cholesky" | custom-call | tf_op jit(solution)/shard_map/jit(cholesky)/cholesky | solution.py:25
  153.7 9.8 %custom-call.65 = f32[1,128,128]{1,2,0:T(8,128)S(1)} custom-call(f32[1,128,128]{2,1,0:T(8,128)S(1)} %get-tuple-element.63), custom_call_target="InvertDiagBlocksLowerTriangular" | custom-call | tf_op jit(solution)/shard_map/jit(cholesky)/cholesky | solution.py:25
  167.0 11.9 %cholesky.487 = f32[128,128]{1,0:T(8,128)S(1)} custom-call(f32[128,128]{1,0:T(8,128)S(1)} %cholesky.594), custom_call_target="Cholesky" | custom-call | tf_op jit(solution)/shard_map/jit(cholesky)/cholesky | solution.py:25
  180.2 9.8 %custom-call.66 = f32[1,128,128]{1,2,0:T(8,128)S(1)} custom-call(f32[1,128,128]{2,1,0:T(8,128)S(1)} %get-tuple-element.60), custom_call_target="InvertDiagBlocksLowerTriangular" | custom-call | tf_op jit(solution)/shard_map/jit(cholesky)/cholesky | solution.py:25
  193.5 11.7 %cholesky.506 = f32[128,128]{1,0:T(8,128)S(1)} custom-call(f32[128,128]{1,0:T(8,128)S(1)} %cholesky.599), custom_call_target="Cholesky" | custom-call | tf_op jit(solution)/shard_map/jit(cholesky)/cholesky | solution.py:25
  206.4 10.2 %custom-call.67 = f32[1,128,128]{1,2,0:T(8,128)S(1)} custom-call(f32[1,128,128]{2,1,0:T(8,128)S(1)} %get-tuple-element.57), custom_call_target="InvertDiagBlocksLowerTriangular" | custom-call | tf_op jit(solution)/shard_map/jit(cholesky)/cholesky | solution.py:25
  219.9 11.7 %cholesky.526 = f32[128,128]{1,0:T(8,128)S(1)} custom-call(f32[128,128]{1,0:T(8,128)S(1)} %cholesky.604), custom_call_target="Cholesky" | custom-call | tf_op jit(solution)/shard_map/jit(cholesky)/cholesky | solution.py:25
  233.0 9.8 %custom-call.68 = f32[1,128,128]{1,2,0:T(8,128)S(1)} custom-call(f32[1,128,128]{2,1,0:T(8,128)S(1)} %get-tuple-element.54), custom_call_target="InvertDiagBlocksLowerTriangular" | custom-call | tf_op jit(solution)/shard_map/jit(cholesky)/cholesky | solution.py:25
  245.8 11.9 %cholesky.546 = f32[128,128]{1,0:T(8,128)S(1)} custom-call(f32[128,128]{1,0:T(8,128)S(1)} %cholesky.609), custom_call_target="Cholesky" | custom-call | tf_op jit(solution)/shard_map/jit(cholesky)/cholesky | solution.py:25
  259.0 9.8 %custom-call.69 = f32[1,128,128]{1,2,0:T(8,128)S(1)} custom-call(f32[1,128,128]{2,1,0:T(8,128)S(1)} %get-tuple-element.51), custom_call_target="InvertDiagBlocksLowerTriangular" | custom-call | tf_op jit(solution)/shard_map/jit(cholesky)/cholesky | solution.py:25
  271.5 11.7 %cholesky.564 = f32[128,128]{1,0:T(8,128)S(1)} custom-call(f32[128,128]{1,0:T(8,128)S(1)} %convolution_subtract_fusion.11), custom_call_target="Cholesky" | custom-call | tf_op jit(solution)/shard_map/jit(cholesky)/cholesky | solution.py:25
  290.3 4.8 select_select_fusion
  295.1 23.4 %while.1 = (s32[]{:T(128)}, f32[1024,1024]{1,0:T(8,128)}, s32[8,2]{0,1:T(2,128)S(1)}, f32[8,128,128]{2,1,0:T(8,128)S(1)}, s32[]{:T(128)}) while((s32[]{:T(128)}, f32[1024,1024]{1,0:T(8,128)}, s32[8,2]{0,1:T(2,128)S(1)}, f32[8,128,128]{2,1,0:T(8,128)S(1)}, s32[]{:T(128)}) %tuple.58), condition=%wide.while_cond, body=%wide.while_body.sunk | while | flops 2 | bytes 131181 | solution.py:27
  318.5 78.8 %custom-call.70 = f32[8,128,128]{1,2,0:T(8,128)S(1)} custom-call(f32[8,128,128]{2,1,0:T(8,128)S(1)} %get-tuple-element.12), custom_call_target="InvertDiagBlocksLowerTriangular" | custom-call | tf_op jit(solution)/shard_map/jit(_solve_triangular)/triangular_solve | solution.py:27
  408.7 2.8 convolution_subtract_fusion.2
  412.2 3.0 convolution_subtract_fusion.1
  415.8 3.7 convolution_subtract_fusion.3
  420.2 28.1 %fusion.79 = f32[1024,2048]{1,0:T(8,128)} fusion(f32[1024,1024]{1,0:T(8,128)S(1)} %convolution_dynamic-update-slice_fusion, f32[1024,2048]{1,0:T(8,128)S(1)} %bitcast.130), kind=kOutput, calls=%fused_computation.177 | convolution fusion | flops 25769803776 | bytes 20971520 | tf_op jit(solution)/shard_map/dot_general | solution.py:15
  453.1 35.0 %fusion = f32[1024,1024]{1,0:T(8,128)S(1)} fusion(f32[2048,1024]{1,0:T(8,128)} %param.8, f32[256,8,8,128]{3,2,1,0:T(8,128)S(1)} %bitcast.122, f32[128,8,16,128]{3,2,1,0:T(8,128)S(1)} %bitcast.121, f32[1024,2048]{1,0:T(8,128)} %fusion.79), kind=kOutput, calls=%fused_computation.3 | convolution fusion | flops 25776095232 | bytes 37748736 | tf_op jit(solution)/shard_map/dot_general | solution.py:15
  488.1 7.0 %convolution_add_fusion = f32[1024,1024]{1,0:T(8,128)} fusion(f32[1024,1024]{1,0:T(8,128)S(1)} %fusion, f32[1024,1024]{1,0:T(8,128)} %get-tuple-element.79, s32[]{:T(128)S(6)} %select_n.19, f32[1024,1024]{1,0:T(8,128)} %copy-done.2, f32[128,1024]{1,0:T(8,128)} %param.9, f32[1024,1024]{1,0:T(8,128)} %get-tuple-element.78), kind=kOutput, calls=%fused_computation.15 | convolution fusion | flops 1611923456 | bytes 10486784 | tf_op jit(solution)/shard_map/dot_general | solution.py:15
  495.2 50.1 %reduce-scatter.2.cloned.1.call-done = f32[128,1024]{1,0:T(8,128)} async-done(((f32[1024,1024]{1,0:T(8,128)}), f32[128,1024]{1,0:T(8,128)}) %reduce-scatter.2.cloned.1.call-update) | async-done | bytes 524304 | tf_op jit(solution)/shard_map/reduce_scatter | solution.py:51
  (106 shorter events, 79.1 us)
Async XLA Ops:
  6.5 5.9 %copy-start.3 = (s32[8,136]{1,0:T(8,128)S(1)}, s32[8,136]{1,0:T(8,128)}, u32[]{:S(2)}) copy-start(s32[8,136]{1,0:T(8,128)} %param.10) | copy-start | bytes 13060
  6.5 68.2 %all-gather.2.cloned.1.call-start = ((), (), s32[]{:S(2)}) async-start(), calls=%async_computation.1 | async-start | bytes 4325376 | tf_op jit(solution)/shard_map/all_gather | solution.py:23
  7.3 538.0 %reduce-scatter.2.cloned.1.call-start = ((), (), s32[]{:S(2)}) async-start(), calls=%async_computation.2 | async-start | bytes 4718592 | tf_op jit(solution)/shard_map/reduce_scatter | solution.py:51
  85.0 2.0 copy-start.1
  397.3 3.2 copy-start
  408.7 11.5 %slice-start = ((s8[8388608]{0:T(1024)(128)(4,1)}), s8[4194304]{0:T(1024)(128)(4,1)S(1)}, s32[]{:S(2)}) async-start(s8[8388608]{0:T(1024)(128)(4,1)} %bitcast.129), calls=%async_computation.3 | async-start | bytes 8388608
  412.2 8.0 %slice-start.1 = ((s8[8388608]{0:T(1024)(128)(4,1)}), s8[4194304]{0:T(1024)(128)(4,1)S(1)}, s32[]{:S(2)}) async-start(s8[8388608]{0:T(1024)(128)(4,1)} %bitcast.129), calls=%async_computation.4 | async-start | bytes 8388608
  420.2 28.1 %copy-start.2 = (f32[1024,1024]{1,0:T(8,128)}, f32[1024,1024]{1,0:T(8,128)S(1)}, u32[]{:S(2)}) copy-start(f32[1024,1024]{1,0:T(8,128)S(1)} %convolution_dynamic-update-slice_fusion) | copy-start | bytes 12582916
Sparse Core Ops, SparseCore 0:
  10.3 64.3 all-gather.1
  495.3 49.9 reduce-scatter.1
where the time goes:
time: 558 us; the launch traced here: 552 us
  other arithmetic  266 us (48%)
  matrix products  116 us (21%)
  waiting for transfers between devices  105 us (19%)
  local copies, waits for them, and re-layouts  46.1 us (8%)
  between operations  19.1 us (3%)
    another operation x30, other arithmetic, per_device(): factor = jnp.linalg.cholesky(gathered)  172 us
    another operation x3, other arithmetic, per_device(): tail_inv = jax.scipy.linalg.solve_triangular(factor, identity, lower=True)  83.7 us
    dot_general x3, matrix products, product(): jnp.dot(left_rows, right_rows, precision=lax.Precision.HIGHEST, preferred...  70.2 us
    all_gather x1, waiting for transfers between devices, per_device(): gathered = lax.all_gather(schur_tail, ('row', 'col'), axis=0, tiled=True)  54.6 us
    reduce_scatter x1, waiting for transfers between devices, per_device(): lax.psum_scatter(product(lead_part, ks_block) + product(diag_cols, tail_b...  50.1 us
    another operation x24, local copies, waits for them, and re-layouts  23.3 us
    another operation x14, matrix products, per_device(): factor = jnp.linalg.cholesky(gathered)  23.1 us
    another operation x15, matrix products, per_device(): tail_inv = jax.scipy.linalg.solve_triangular(factor, identity, lower=True)  22.7 us
  transfers between devices with their start and end apart: 2, of which 2 were waited for; matrix products, arithmetic and copies ran while one was open for 2% of the time, Pallas kernels for 0%

commit v1 on v0

--- a/solution.py
+++ b/solution.py
@@ -1,9 +1,12 @@
 import jax
 import jax.numpy as jnp
 from jax import lax
+from jax.experimental import pallas as pl
+from jax.experimental.pallas import tpu as pltpu
 from jax.sharding import PartitionSpec as P
 
 BLK = 128
+SUB = 8
 
 
 def expand(block_mask):
@@ -13,8 +16,137 @@
 
 def product(left_rows, right_rows):
     return jnp.dot(
-        left_rows, right_rows, precision=lax.Precision.HIGHEST, preferred_element_type=jnp.float32
+        left_rows, right_rows, precision=lax.Precision.HIGH, preferred_element_type=jnp.float32
     )
+
+
+def split3(x):
+    high = x.astype(jnp.bfloat16)
+    rest = x - high.astype(jnp.float32)
+    mid = rest.astype(jnp.bfloat16)
+    low = (rest - mid.astype(jnp.float32)).astype(jnp.bfloat16)
+    return high, mid, low
+
+
+def dot_t(a, b):
+    return lax.dot_general(a, b, (((0,), (0,)), ((), ())), preferred_element_type=jnp.float32)
+
+
+def invert_block(block):
+    lane = lax.broadcasted_iota(jnp.int32, (SUB, BLK), 1)
+    sub = lax.broadcasted_iota(jnp.int32, (SUB, BLK), 0)
+    count = BLK // SUB
+    groups = [block[g * SUB : (g + 1) * SUB, :] for g in range(count)]
+    done = []
+
+    def spread(x, j):
+        return jnp.broadcast_to(x[:, j : j + 1], (SUB, BLK))
+
+    def pick(x, s):
+        return jnp.broadcast_to(x[s : s + 1, :], (SUB, BLK))
+
+    for g in range(count):
+        base = g * SUB
+        columns = [spread(groups[g], base + c) for c in range(SUB)]
+        others = {h: [spread(groups[h], base + c) for c in range(SUB)] for h in range(g + 1, count)}
+        rows = groups[g]
+        final = jnp.zeros((SUB, BLK), jnp.float32)
+        for s in range(SUB):
+            pivot = pick(columns[s], s)
+            inverse = 1.0 / pivot
+            unit = jnp.where(lane == base + s, 1.0, pick(rows, s))
+            final = jnp.where(sub == s, unit * lax.rsqrt(pivot), final)
+            scaled = unit * inverse
+            rows = jnp.where(
+                sub == s, scaled, jnp.where(lane == base + s, 0.0, rows) - columns[s] * scaled
+            )
+            for c in range(s + 1, SUB):
+                part = pick(columns[c], s) * inverse
+                columns[c] = jnp.where(sub == s, part, columns[c] - columns[s] * part)
+        spreads = [pick(rows, c) for c in range(SUB)]
+        inside = (lane >= base) & (lane < base + SUB)
+        for h in range(g + 1, count):
+            first = others[h][0] * spreads[0] + others[h][1] * spreads[1]
+            second = others[h][2] * spreads[2] + others[h][3] * spreads[3]
+            third = others[h][4] * spreads[4] + others[h][5] * spreads[5]
+            fourth = others[h][6] * spreads[6] + others[h][7] * spreads[7]
+            groups[h] = jnp.where(inside, 0.0, groups[h]) - ((first + second) + (third + fourth))
+        done.append(jnp.where(lane <= sub + base, final, 0.0))
+    return jnp.concatenate(done, axis=0)
+
+
+def inverse_kernel(a_ref, out_ref, tri_ref, wide_ref, sem):
+    size = a_ref.shape[0]
+    count = size // BLK
+    copy = pltpu.make_async_copy(a_ref, out_ref, sem)
+    copy.start()
+    copy.wait()
+
+    def step(k, carry):
+        here = pl.ds(pl.multiple_of(k * BLK, BLK), BLK)
+        inverse = invert_block(out_ref[here, here])
+        out_ref[here, here] = jnp.zeros((BLK, BLK), jnp.float32)
+        ih, im, il = split3(inverse)
+        row = out_ref[here, :]
+        rh, rm, rl = split3(row)
+        left = jnp.concatenate([ih, im], axis=1)
+        last = jnp.concatenate([ih, il], axis=1)
+        new = (
+            jnp.dot(last, jnp.concatenate([rl, rh], axis=0), preferred_element_type=jnp.float32)
+            + jnp.dot(left, jnp.concatenate([rm, rm], axis=0), preferred_element_type=jnp.float32)
+            + jnp.dot(left, jnp.concatenate([rh, rh], axis=0), preferred_element_type=jnp.float32)
+        )
+        out_ref[here, :] = new
+        out_ref[here, here] = inverse
+        full = out_ref[here, :]
+        fh, fm, fl = split3(full)
+        wide_ref[0:BLK, :] = fh
+        wide_ref[BLK : 2 * BLK, :] = fm
+        wide_ref[2 * BLK :, :] = fl
+
+        def below(i, inner):
+            there = pl.ds(pl.multiple_of(i * BLK, BLK), BLK)
+            out_ref[there, here] = jnp.zeros((BLK, BLK), jnp.float32)
+            ph, pm, plow = wide_ref[0:BLK, there], wide_ref[BLK : 2 * BLK, there], wide_ref[2 * BLK :, there]
+            fh, fm, fl = wide_ref[0:BLK, :], wide_ref[BLK : 2 * BLK, :], wide_ref[2 * BLK :, :]
+            left = jnp.concatenate([ph, pm], axis=0)
+            last = jnp.concatenate([ph, plow], axis=0)
+            change = (
+                dot_t(last, jnp.concatenate([fl, fh], axis=0))
+                + dot_t(left, jnp.concatenate([fm, fm], axis=0))
+                + dot_t(left, jnp.concatenate([fh, fh], axis=0))
+            )
+            out_ref[there, :] = out_ref[there, :] - change
+            return inner
+
+        lax.fori_loop(k + 1, count, below, 0)
+        return carry
+
+    lax.fori_loop(0, count, step, 0)
+
+    def clear(k, carry):
+        here = pl.ds(pl.multiple_of(k * BLK, BLK), BLK)
+        lane = lax.broadcasted_iota(jnp.int32, (BLK, size), 1)
+        out_ref[here, :] = jnp.where(lane < (k + 1) * BLK, out_ref[here, :], 0.0)
+        return carry
+
+    lax.fori_loop(0, count, clear, 0)
+
+
+def factor_inverse(gathered):
+    size = gathered.shape[0]
+    return pl.pallas_call(
+        inverse_kernel,
+        out_shape=jax.ShapeDtypeStruct((size, size), jnp.float32),
+        in_specs=[pl.BlockSpec(memory_space=pl.ANY)],
+        out_specs=pl.BlockSpec(memory_space=pltpu.VMEM),
+        scratch_shapes=[
+            pltpu.VMEM((8, BLK), jnp.float32),
+            pltpu.VMEM((3 * BLK, size), jnp.bfloat16),
+            pltpu.SemaphoreType.DMA(()),
+        ],
+        name="factor_inverse",
+    )(gathered)
 
 
 def per_device(schur_tail, coupling, ks_lead, ks_tail, inv_mask, ks_mask):
@@ -22,9 +154,7 @@
     col_index = lax.axis_index("col")
     gathered = lax.all_gather(schur_tail, ("row", "col"), axis=0, tiled=True)
     tail_size = gathered.shape[0]
-    factor = jnp.linalg.cholesky(gathered)
-    identity = jnp.eye(tail_size, dtype=jnp.float32)
-    tail_inv = jax.scipy.linalg.solve_triangular(factor, identity, lower=True)
+    tail_inv = factor_inverse(gathered)
     lead_width = coupling.shape[1]
     lead_blocks = lead_width // BLK
     col_width = ks_lead.shape[1]

time: 558 us -> 247 us (0.44)
  other arithmetic: 266 us -> 2.92 us
  matrix products: 116 us -> 47.9 us
  Pallas kernels: 0 us -> 57.8 us
  local copies, waits for them, and re-layouts: 46.1 us -> 16.7 us
  between operations: 19.1 us -> 13.5 us
    another operation x33 -> x0, other arithmetic: 256 us -> none  [the longest x30 172 us: per_device(): factor = jnp.linalg.cholesky(gathered)]
    pallas_call x0 -> x1, Pallas kernels: none -> 57.8 us  [factor_inverse(): pl.pallas_call(inverse_kernel, out_shape=jax.ShapeDtypeStruct((size, size...]
    another operation x29 -> x0, matrix products: 45.8 us -> none  [the longest x14 23.1 us: per_device(): factor = jnp.linalg.cholesky(gathered)]
    another operation x33 -> x0, local copies, waits for them, and re-layouts: 25.8 us -> none
    dot_general x3, matrix products: 70.2 us -> 47.9 us  [product(): jnp.dot(left_rows, right_rows, precision=lax.Precision.HIGH, preferred_el...]
    all_gather x1 -> x0, local copies, waits for them, and re-layouts: 5.85 us -> none  [per_device(): gathered = lax.all_gather(schur_tail, ('row', 'col'), axis=0, tiled=True)]
  transfers between devices with their start and end apart: 2 -> 2, of which waited for: 2 -> 2; matrix products, arithmetic and copies ran while one was open for 2% -> 4% of each run, Pallas kernels for 0% -> 0%
where the time goes in v1:
time: 247 us; the launch traced here: 246 us
  waiting for transfers between devices  107 us (43%)
  Pallas kernels  57.8 us (23%)
  matrix products  47.9 us (19%)
  local copies, waits for them, and re-layouts  16.7 us (7%)
  between operations  13.5 us (5%)
  other arithmetic  2.92 us (1%)
    pallas_call x1, Pallas kernels, factor_inverse(): pl.pallas_call(inverse_kernel, out_shape=jax.ShapeDtypeStruct((size, size...  57.8 us
    all_gather x1, waiting for transfers between devices, per_device(): gathered = lax.all_gather(schur_tail, ('row', 'col'), axis=0, tiled=True)  56.6 us
    reduce_scatter x1, waiting for transfers between devices, per_device(): lax.psum_scatter(product(lead_part, ks_block) + product(diag_cols, tail_b...  50.1 us
    dot_general x3, matrix products, product(): jnp.dot(left_rows, right_rows, precision=lax.Precision.HIGH, preferred_el...  47.9 us
    broadcast_in_dim x4, local copies, waits for them, and re-layouts, expand(): return jnp.repeat(widened, BLK, axis=1)  11 us
    reshape x1, local copies, waits for them, and re-layouts, expand(): return jnp.repeat(widened, BLK, axis=1)  5.35 us
  transfers between devices with their start and end apart: 2, of which 2 were waited for; matrix products, arithmetic and copies ran while one was open for 4% of the time, Pallas kernels for 0%

profile of v1, /device:TPU:0, one launch (start us, length us, event | category | flops | bytes accessed | tf_op | source)
XLA Modules:
  0.0 246.3 jit_solution(12632805735865019001)
XLA Ops:
  6.5 0.0 all-gather.2.cloned.1.call-start
  6.5 0.7 all-gather.2.cloned.1.call-update
  7.3 0.0 reduce-scatter.2.cloned.1.call-start
  7.3 0.8 dynamic-slice_convert_fusion.1
  8.1 0.1 copy.7
  8.2 0.7 dynamic-slice_convert_fusion
  8.9 0.1 copy.8
  8.9 0.8 dynamic-slice_convert_fusion.2
  9.7 0.7 slice_convert_fusion
  10.4 1.1 broadcast_in_dim.31
  11.6 1.1 broadcast_in_dim.29
  12.7 5.4 %copy_bitcast_fusion = (f32[1024,1024]{1,0:T(8,128)}, f32[1024,1024]{1,0:T(8,128)}) fusion(f32[128,8,8,128]{3,2,1,0:T(8,128)S(1)} %bitcast.22, f32[128,8,8,128]{3,2,1,0:T(8,128)S(1)} %bitcast.23), kind=kLoop, calls=%fused_computation.6 | loop fusion | bytes 16777216 | tf_op jit(solution)/shard_map/reshape | solution.py:14
  18.1 56.6 %all-gather.2.cloned.1.call-done.a_ref = f32[1024,1024]{1,0:T(8,128)} async-done(((f32[32,1024]{1,0:T(8,128)}), f32[1024,1024]{1,0:T(8,128)}) %all-gather.2.cloned.1.call-update) | async-done | bytes 4194320 | tf_op jit(solution)/shard_map/all_gather | solution.py:155
  74.7 57.8 %factor_inverse.1 = f32[1024,1024]{1,0:T(8,128)} custom-call(f32[1024,1024]{1,0:T(8,128)} %all-gather.2.cloned.1.call-done.a_ref), custom_call_target="tpu_custom_call" | custom-call | tf_op jit(solution)/shard_map/factor_inverse/pallas_call | solution.py:138
  132.6 18.0 %fusion.8 = f32[1024,2048]{1,0:T(8,128)} fusion(f32[1024,1024]{1,0:T(8,128)} %factor_inverse.1, f32[1024,2048]{1,0:T(8,128)} %param.7), kind=kOutput, calls=%fused_computation.18 | convolution fusion | flops 12884901888 | bytes 20971520 | tf_op jit(solution)/shard_map/dot_general | solution.py:18
  150.6 0.1 broadcast_in_dim.26
  150.7 6.4 %broadcast_in_dim.27 = f32[2048,8,128]{2,1,0:T(8,128)} broadcast(f32[2048,8]{1,0:T(8,128)S(1)} %bitcast.24), dimensions={0,1} | broadcast | bytes 8454144 | tf_op jit(solution)/shard_map/broadcast_in_dim | solution.py:14
  157.1 2.3 broadcast_in_dim.25
  159.4 0.0 copy-start
  159.4 23.4 %fusion = f32[1024,1024]{1,0:T(8,128)} fusion(f32[2048,1024]{1,0:T(8,128)} %param.8, f32[256,8,8,128]{3,2,1,0:T(8,128)} %bitcast.21, f32[128,8,16,128]{3,2,1,0:T(8,128)S(1)} %bitcast.20, f32[1024,2048]{1,0:T(8,128)} %fusion.8), kind=kOutput, calls=%fused_computation.1 | convolution fusion | flops 12891193344 | bytes 37748736 | tf_op jit(solution)/shard_map/dot_general | solution.py:18
  182.9 0.0 copy-done
  182.9 6.4 %convolution_add_fusion = f32[1024,1024]{1,0:T(8,128)} fusion(f32[1024,1024]{1,0:T(8,128)} %fusion, f32[1024,1024]{1,0:T(8,128)} %get-tuple-element.6, s32[]{:T(128)S(6)} %select_n.14, f32[1024,1024]{1,0:T(8,128)} %factor_inverse.1, f32[128,1024]{1,0:T(8,128)S(1)} %copy-done, f32[1024,1024]{1,0:T(8,128)} %get-tuple-element.5), kind=kOutput, calls=%fused_computation.8 | convolution fusion | flops 806617088 | bytes 10486784 | tf_op jit(solution)/shard_map/dot_general | solution.py:18
  189.3 0.0 reduce-scatter.2.cloned.1.call-update
  189.3 50.1 %reduce-scatter.2.cloned.1.call-done = f32[128,1024]{1,0:T(8,128)} async-done(((f32[1024,1024]{1,0:T(8,128)}), f32[128,1024]{1,0:T(8,128)}) %reduce-scatter.2.cloned.1.call-update) | async-done | bytes 524304 | tf_op jit(solution)/shard_map/reduce_scatter | solution.py:181
  (3 shorter events, 0.1 us)
Async XLA Ops:
  6.5 68.2 %all-gather.2.cloned.1.call-start = ((), (), s32[]{:S(2)}) async-start(), calls=%async_computation.1 | async-start | bytes 4325376 | tf_op jit(solution)/shard_map/all_gather | solution.py:155
  7.3 232.2 %reduce-scatter.2.cloned.1.call-start = ((), (), s32[]{:S(2)}) async-start(), calls=%async_computation.2 | async-start | bytes 4718592 | tf_op jit(solution)/shard_map/reduce_scatter | solution.py:181
  159.4 23.4 %copy-start = (f32[128,1024]{1,0:T(8,128)S(1)}, f32[128,1024]{1,0:T(8,128)}, u32[]{:S(2)}) copy-start(f32[128,1024]{1,0:T(8,128)} %param.9) | copy-start | bytes 1572868
Sparse Core Ops, SparseCore 0:
  10.3 64.3 all-gather.1
  189.4 49.9 reduce-scatter.1

commit v2 on v1

--- a/solution.py
+++ b/solution.py
@@ -1,3 +1,5 @@
+import functools
+
 import jax
 import jax.numpy as jnp
 from jax import lax
@@ -5,6 +7,7 @@
 from jax.experimental.pallas import tpu as pltpu
 from jax.sharding import PartitionSpec as P
 
+MESH = pl.DeviceIdType.MESH
 BLK = 128
 SUB = 8
 
@@ -149,10 +152,151 @@
     )(gathered)
 
 
-def per_device(schur_tail, coupling, ks_lead, ks_tail, inv_mask, ks_mask):
+def greet(peers):
+    barrier = pltpu.get_barrier_semaphore()
+    for peer in peers:
+        pl.semaphore_signal(barrier, inc=1, device_id=peer, device_id_type=MESH)
+    pl.semaphore_wait(barrier, len(peers))
+
+
+def gather_kernel(rows, cols, x_ref, out_ref, send1, recv1, send2, recv2, send3, recv3):
+    me_row, me_col = lax.axis_index("row"), lax.axis_index("col")
+    chips = rows // 2
+    chip, core = lax.div(me_row, 2), lax.rem(me_row, 2)
+    part = x_ref.shape[0]
+    whole = part * cols
+
+    def at_chip(q):
+        return q * 2 + core
+
+    partner = (chip * 2 + 1 - core, me_col)
+    col_peers = [(me_row, lax.rem(me_col + d, cols)) for d in range(1, cols)]
+    chip_peers = [(at_chip(lax.rem(chip + d, chips)), me_col) for d in range(1, chips)]
+    greet(col_peers + chip_peers + [partner])
+
+    mine = out_ref.at[pl.ds(pl.multiple_of((me_row * cols + me_col) * part, SUB), part)]
+    first = []
+    for d in range(1, cols):
+        copy = pltpu.make_async_remote_copy(
+            x_ref, mine, send1.at[d - 1], recv1.at[d - 1], device_id=col_peers[d - 1], device_id_type=MESH
+        )
+        copy.start()
+        first.append(copy)
+    mine[...] = x_ref[...]
+    for copy in first:
+        copy.wait_recv()
+
+    def block(row):
+        return out_ref.at[pl.ds(pl.multiple_of(row * whole, SUB), whole)]
+
+    def forward(row, slot):
+        copy = pltpu.make_async_remote_copy(
+            block(row), block(row), send3.at[slot], recv3.at[slot], device_id=partner, device_id_type=MESH
+        )
+        copy.start()
+        return copy
+
+    second = []
+    for d in range(1, chips):
+        copy = pltpu.make_async_remote_copy(
+            block(me_row), block(me_row), send2.at[d - 1], recv2.at[d - 1],
+            device_id=chip_peers[d - 1], device_id_type=MESH,
+        )
+        copy.start()
+        second.append(copy)
+    third = [forward(me_row, 0)]
+    for d in range(1, chips):
+        second[d - 1].wait_recv()
+        third.append(forward(at_chip(lax.rem(chip + chips - d, chips)), d))
+    for copy in third:
+        copy.wait_recv()
+    for copy in first + second + third:
+        copy.wait_send()
+
+
+def gather(part, mesh_rows, mesh_cols):
+    dma = pltpu.SemaphoreType.DMA
+    chips = mesh_rows // 2
+    return pl.pallas_call(
+        functools.partial(gather_kernel, mesh_rows, mesh_cols),
+        out_shape=jax.ShapeDtypeStruct((part.shape[0] * mesh_rows * mesh_cols, part.shape[1]), jnp.float32),
+        in_specs=[pl.BlockSpec(memory_space=pltpu.VMEM)],
+        out_specs=pl.BlockSpec(memory_space=pltpu.VMEM),
+        scratch_shapes=[
+            dma((mesh_cols - 1,)), dma((mesh_cols - 1,)),
+            dma((chips - 1,)), dma((chips - 1,)),
+            dma((chips,)), dma((chips,)),
+        ],
+        compiler_params=pltpu.CompilerParams(collective_id=0, has_side_effects=True),
+        name="gather_tail",
+    )(part)
+
+
+def scatter_kernel(rows, p_ref, out_ref, pair_ref, far_ref, send1, recv1, send2, recv2):
+    me_row, me_col = lax.axis_index("row"), lax.axis_index("col")
+    chips = rows // 2
+    chip, core = lax.div(me_row, 2), lax.rem(me_row, 2)
+    part = out_ref.shape[0]
+    partner = (chip * 2 + 1 - core, me_col)
+    targets = [lax.rem(chip + d, chips) for d in range(chips)]
+    chip_peers = [(targets[d] * 2 + core, me_col) for d in range(1, chips)]
+    greet(chip_peers + [partner])
+
+    def block(row):
+        return p_ref.at[pl.ds(pl.multiple_of(row * part, SUB), part)]
+
+    order = list(range(1, chips)) + [0]
+    first = {}
+    for d in order:
+        copy = pltpu.make_async_remote_copy(
+            block(targets[d] * 2 + 1 - core), pair_ref.at[d], send1.at[d], recv1.at[d],
+            device_id=partner, device_id_type=MESH,
+        )
+        copy.start()
+        first[d] = copy
+    second = []
+    for d in range(1, chips):
+        first[d].wait_recv()
+        pair_ref[d] = pair_ref[d] + block(targets[d] * 2 + core)[...]
+        copy = pltpu.make_async_remote_copy(
+            pair_ref.at[d], far_ref.at[d - 1], send2.at[d - 1], recv2.at[d - 1],
+            device_id=chip_peers[d - 1], device_id_type=MESH,
+        )
+        copy.start()
+        second.append(copy)
+    first[0].wait_recv()
+    out_ref[...] = pair_ref[0] + block(me_row)[...]
+    for d in range(1, chips):
+        second[d - 1].wait_recv()
+        out_ref[...] += far_ref[d - 1]
+    for copy in list(first.values()) + second:
+        copy.wait_send()
+
+
+def scatter_sum(partial, mesh_rows):
+    dma = pltpu.SemaphoreType.DMA
+    chips = mesh_rows // 2
+    part, width = partial.shape[0] // mesh_rows, partial.shape[1]
+    return pl.pallas_call(
+        functools.partial(scatter_kernel, mesh_rows),
+        out_shape=jax.ShapeDtypeStruct((part, width), jnp.float32),
+        in_specs=[pl.BlockSpec(memory_space=pltpu.VMEM)],
+        out_specs=pl.BlockSpec(memory_space=pltpu.VMEM),
+        scratch_shapes=[
+            pltpu.VMEM((chips, part, width), jnp.float32),
+            pltpu.VMEM((chips - 1, part, width), jnp.float32),
+            dma((chips,)), dma((chips,)),
+            dma((chips - 1,)), dma((chips - 1,)),
+        ],
+        compiler_params=pltpu.CompilerParams(collective_id=1, has_side_effects=True),
+        name="scatter_sum",
+    )(partial)
+
+
+def per_device(mesh_rows, mesh_cols, schur_tail, coupling, ks_lead, ks_tail, inv_mask, ks_mask):
     row_index = lax.axis_index("row")
     col_index = lax.axis_index("col")
-    gathered = lax.all_gather(schur_tail, ("row", "col"), axis=0, tiled=True)
+    gathered = gather(schur_tail, mesh_rows, mesh_cols)
     tail_size = gathered.shape[0]
     tail_inv = factor_inverse(gathered)
     lead_width = coupling.shape[1]
@@ -178,17 +322,13 @@
     own_tail_mask = lax.dynamic_slice_in_dim(tail_ks_mask, row_index * tail_rows, tail_rows, 0)
     tail_block = ks_tail * own_tail_mask
     diag_cols = lax.dynamic_slice_in_dim(masked_inv, row_index * tail_rows, tail_rows, 1)
-    return lax.psum_scatter(
-        product(lead_part, ks_block) + product(diag_cols, tail_block),
-        "row",
-        scatter_dimension=0,
-        tiled=True,
-    )
+    partial = product(lead_part, ks_block) + product(diag_cols, tail_block)
+    return scatter_sum(partial, mesh_rows)
 
 
 def solution(mesh):
     in_specs = (P(("row", "col"), None), P(None, "row"), P("row", "col"), P("row", "col"), P(), P())
     out_specs = P("row", "col")
     return jax.shard_map(
-        per_device, mesh=mesh, in_specs=in_specs, out_specs=out_specs, check_vma=False
+        functools.partial(per_device, mesh.shape["row"], mesh.shape["col"]), mesh=mesh, in_specs=in_specs, out_specs=out_specs, check_vma=False
     )

time: 247 us -> 201 us (0.81)
  waiting for transfers between devices: 107 us -> 0 us
  Pallas kernels: 57.8 us -> 134 us
  between operations: 13.5 us -> 0.11 us
  local copies, waits for them, and re-layouts: 16.7 us -> 19.2 us
    pallas_call x0 -> x2, Pallas kernels: none -> 75.8 us  [the longest x1 43.7 us: gather(): pl.pallas_call(functools.partial(gather_kernel, mesh_rows, mesh_cols), ou...]
    all_gather x1 -> x0, waiting for transfers between devices: 56.6 us -> none  [per_device(): gathered = lax.all_gather(schur_tail, ('row', 'col'), axis=0, tiled=True)]
    reduce_scatter x1 -> x0, waiting for transfers between devices: 50.1 us -> none  [per_device(): lax.psum_scatter(product(lead_part, ks_block) + product(diag_cols, tail_b...]
    broadcast_in_dim x4, local copies, waits for them, and re-layouts: 11 us -> 14.7 us  [expand(): return jnp.repeat(widened, BLK, axis=1)]
    reshape x1, local copies, waits for them, and re-layouts: 5.35 us -> 2.17 us  [expand(): return jnp.repeat(widened, BLK, axis=1)]
  transfers between devices with their start and end apart: 2 -> 0, of which waited for: 2 -> 0; matrix products, arithmetic and copies ran while one was open for 4% -> 0% of each run, Pallas kernels for 0% -> 0%
where the time goes in v2:
time: 201 us; the launch traced here: 200 us
  Pallas kernels  134 us (67%)
  matrix products  46 us (23%)
  local copies, waits for them, and re-layouts  19.2 us (10%)
    pallas_call x1, Pallas kernels, factor_inverse(): pl.pallas_call(inverse_kernel, out_shape=jax.ShapeDtypeStruct((size, size...  57.8 us
    dot_general x3, matrix products, product(): jnp.dot(left_rows, right_rows, precision=lax.Precision.HIGH, preferred_el...  46 us
    pallas_call x1, Pallas kernels, gather(): pl.pallas_call(functools.partial(gather_kernel, mesh_rows, mesh_cols), ou...  43.7 us
    pallas_call x1, Pallas kernels, scatter_sum(): pl.pallas_call(functools.partial(scatter_kernel, mesh_rows), out_shape=ja...  32.1 us
    broadcast_in_dim x4, local copies, waits for them, and re-layouts, expand(): return jnp.repeat(widened, BLK, axis=1)  14.7 us

profile of v2, /device:TPU:0, one launch (start us, length us, event | category | flops | bytes accessed | tf_op | source)
XLA Modules:
  0.0 200.5 jit_solution(1187827843100115096)
XLA Ops:
  0.0 0.8 dynamic-slice_convert_fusion.1
  0.8 0.1 copy.7
  0.8 0.1 broadcast_in_dim.26
  0.9 0.0 copy-start.2
  0.9 6.4 %broadcast_in_dim.27 = f32[2048,8,128]{2,1,0:T(8,128)} broadcast(f32[2048,8]{1,0:T(8,128)S(1)} %bitcast.24), dimensions={0,1} | broadcast | bytes 8454144 | tf_op jit(solution)/shard_map/broadcast_in_dim | solution.py:17
  7.3 0.0 copy-done.2
  7.3 0.1 dynamic-slice_convert_fusion.2
  7.4 6.0 %broadcast_in_dim.25 = f32[1024,16,128]{2,1,0:T(8,128)} broadcast(f32[1024,16]{1,0:T(8,128)S(1)} %bitcast.25), dimensions={0,1} | broadcast | bytes 8454144 | tf_op jit(solution)/shard_map/broadcast_in_dim | solution.py:17
  13.5 43.7 %gather_tail.1.a_ref = f32[1024,1024]{1,0:T(8,128)} custom-call(f32[32,1024]{1,0:T(8,128)} %x_ref.1), custom_call_target="tpu_custom_call" | custom-call | tf_op jit(solution)/shard_map/gather_tail/pallas_call | solution.py:220
  57.1 57.8 %factor_inverse.1 = f32[1024,1024]{1,0:T(8,128)} custom-call(f32[1024,1024]{1,0:T(8,128)} %gather_tail.1.a_ref), custom_call_target="tpu_custom_call" | custom-call | tf_op jit(solution)/shard_map/factor_inverse/pallas_call | solution.py:141
  115.0 16.7 %fusion.8 = f32[1024,2048]{1,0:T(8,128)S(1)} fusion(f32[1024,1024]{1,0:T(8,128)} %factor_inverse.1, f32[1024,2048]{1,0:T(8,128)} %param.7), kind=kOutput, calls=%fused_computation.18 | convolution fusion | flops 12884901888 | bytes 20971520 | tf_op jit(solution)/shard_map/dot_general | solution.py:21
  131.7 24.3 %fusion = f32[1024,1024]{1,0:T(8,128)} fusion(f32[2048,1024]{1,0:T(8,128)} %param.8, f32[256,8,8,128]{3,2,1,0:T(8,128)} %bitcast.21, f32[128,8,16,128]{3,2,1,0:T(8,128)} %bitcast.20, f32[1024,2048]{1,0:T(8,128)S(1)} %fusion.8), kind=kOutput, calls=%fused_computation.1 | convolution fusion | flops 12891193344 | bytes 37748736 | tf_op jit(solution)/shard_map/dot_general | solution.py:21
  156.1 0.7 dynamic-slice_convert_fusion
  156.8 0.1 copy.8
  156.9 1.1 broadcast_in_dim.31
  158.1 1.1 broadcast_in_dim.29
  159.2 0.0 copy-start
  159.2 0.0 copy-start.1
  159.2 2.2 %copy_bitcast_fusion = (f32[1024,1024]{1,0:T(8,128)S(1)}, f32[1024,1024]{1,0:T(8,128)S(1)}) fusion(f32[128,8,8,128]{3,2,1,0:T(8,128)S(1)} %bitcast.22, f32[128,8,8,128]{3,2,1,0:T(8,128)S(1)} %bitcast.23), kind=kLoop, calls=%fused_computation.6 | loop fusion | bytes 16777216 | tf_op jit(solution)/shard_map/reshape | solution.py:17
  161.4 0.0 copy-done
  161.4 0.1 copy-done.1
  161.5 5.0 %convolution_add_fusion.p_ref = f32[1024,1024]{1,0:T(8,128)} fusion(f32[1024,1024]{1,0:T(8,128)S(1)} %copy-done, f32[1024,1024]{1,0:T(8,128)S(1)} %get-tuple-element.6, s32[]{:T(128)S(6)} %select_n.14, f32[1024,1024]{1,0:T(8,128)} %factor_inverse.1, f32[128,1024]{1,0:T(8,128)S(1)} %copy-done.1, f32[1024,1024]{1,0:T(8,128)S(1)} %get-tuple-element.5), kind=kOutput, calls=%fused_computation.8 | convolution fusion | flops 806617088 | bytes 10486784 | tf_op jit(solution)/shard_map/dot_general | solution.py:21
  166.5 32.1 %scatter_sum.1 = f32[128,1024]{1,0:T(8,128)} custom-call(f32[1024,1024]{1,0:T(8,128)} %convolution_add_fusion.p_ref), custom_call_target="tpu_custom_call" | custom-call | tf_op jit(solution)/shard_map/scatter_sum/pallas_call | solution.py:280
  198.6 1.9 copy.24
  (4 shorter events, 0.1 us)
Async XLA Ops:
  0.9 6.4 %copy-start.2 = (s32[8,136]{1,0:T(8,128)S(1)}, s32[8,136]{1,0:T(8,128)}, u32[]{:S(2)}) copy-start(s32[8,136]{1,0:T(8,128)} %param.10) | copy-start | bytes 13060
  159.2 2.2 %copy-start = (f32[1024,1024]{1,0:T(8,128)S(1)}, f32[1024,1024]{1,0:T(8,128)}, u32[]{:S(2)}) copy-start(f32[1024,1024]{1,0:T(8,128)} %fusion) | copy-start | bytes 12582916
  159.2 2.3 %copy-start.1 = (f32[128,1024]{1,0:T(8,128)S(1)}, f32[128,1024]{1,0:T(8,128)}, u32[]{:S(2)}) copy-start(f32[128,1024]{1,0:T(8,128)} %param.9) | copy-start | bytes 1572868
